TPU v7x, 32 devices: a whole 2x2x4 slice. The times are simulated.
32 devices in a mesh: rep: 1, fsdp: 32 (over z, y, x, core).
Axes of the slice: x: 2, y: 2, z: 4, core: 2. Of those that a mesh axis runs over, the one named last changes fastest.
Arguments:
- grads: bfloat16 [1, 24, 1280, 1280], P('rep', None, 'fsdp'), as said below
- group_counts: int32 [2], replicated, may hold values from 1 to 18, 24 in all
- owners: int32 [24], replicated, may hold values from 0 to 31, as said below
- left_stat: float32 [32, 1280, 1280], P('fsdp', 'rep'), may hold values from -4 to 4
- right_stat: float32 [32, 1280, 1280], P('fsdp', 'rep'), may hold values from -4 to 4
- left_root: bfloat16 [32, 1280, 1280], P('fsdp', 'rep'), as said below
- right_root: bfloat16 [32, 1280, 1280], P('fsdp', 'rep'), as said below
Outputs:
- left_new: float32 [32, 1280, 1280], P('fsdp', 'rep')
- right_new: float32 [32, 1280, 1280], P('fsdp', 'rep')
- update: bfloat16 [24, 1280, 1280], P(None, ('rep', 'fsdp'))
Inputs may be any that keep to these rules, and one draw needn't show every extreme that they name: `grads`: block gradients of every replica group, real-valued. `owners`: no slot is named by two blocks. `group_counts`: the counts add up to 24. `left_root`: Symmetric, with a positive diagonal of about 0.5 to 2, each entry within a small symmetric perturbation of that range, and off-diagonal entries much smaller than the diagonal. `right_root`: Symmetric, with a positive diagonal of about 0.5 to 2, each entry within a small symmetric perturbation of that range, and off-diagonal entries much smaller than the diagonal.
All inputs are finite; a program needn't handle non-finite values.
Results may differ from a plain program's by a relative error of at most 0.00065.
The roundings to bfloat16 on the way count: a program that leaves them out, or rounds other values in their place, can miss the bound.
Values may be sent and summed in bfloat16 or wider, within the bound.
A program may use at most 128 MiB of HBM per device.

v0:
```python
import jax
import jax.numpy as jnp
from jax import lax
from jax.sharding import PartitionSpec as P

BETA = 0.95
EPSILON = 1e-06


def on_device(grads, group_counts, owners, left_stat, right_stat, left_root, right_root):
    slots = lax.axis_size("fsdp")
    width = left_stat.shape[2]
    half_rows = left_stat.shape[1]
    slot_ids = jnp.arange(slots, dtype=jnp.int32)
    placing = (owners[:, None] == slot_ids[None, :]).astype(jnp.bfloat16)
    local = grads[0]
    summed = lax.psum(local, "rep").astype(jnp.float32).astype(jnp.bfloat16)
    slotted = jnp.einsum("bs,brc->src", placing, summed, preferred_element_type=jnp.float32).astype(
        jnp.bfloat16
    )
    block = lax.all_to_all(slotted, "fsdp", split_axis=0, concat_axis=1, tiled=True)[0]
    first = lax.axis_index("rep") * half_rows
    mine = lax.dynamic_slice_in_dim(block, first, half_rows, 0)
    columns = lax.dynamic_slice_in_dim(block, first, half_rows, 1)
    coef = (1.0 - BETA) / width
    left_gram = jnp.dot(mine, block.T, preferred_element_type=jnp.float32)
    right_gram = lax.dot_general(
        columns, block, (((0,), (0,)), ((), ())), preferred_element_type=jnp.float32
    )
    left_new = BETA * left_stat[0] + coef * left_gram
    right_new = BETA * right_stat[0] + coef * right_gram
    whole_root = lax.all_gather(right_root, "rep", axis=1, tiled=True)[0]
    halfway = jnp.dot(left_root[0], block, preferred_element_type=jnp.float32).astype(jnp.bfloat16)
    precond = jnp.dot(halfway, whole_root, preferred_element_type=jnp.float32)
    ends = jnp.cumsum(group_counts)
    starts = ends - group_counts
    block_ids = jnp.arange(owners.shape[0], dtype=jnp.int32)
    member = (
        (block_ids[:, None] >= starts[None, :]) & (block_ids[:, None] < ends[None, :])
    ).astype(jnp.float32)
    owned_here = (owners == lax.axis_index("fsdp")).astype(jnp.float32)
    my_groups = jnp.sum(owned_here[:, None] * member, axis=0)
    mine_float = mine.astype(jnp.float32)
    grad_part = my_groups * jnp.sum(mine_float * mine_float)
    prec_part = my_groups * jnp.sum(precond * precond)
    grad_sq, prec_sq = lax.psum((grad_part, prec_part), ("rep", "fsdp"))
    ratio = jnp.sum(my_groups * jnp.sqrt((grad_sq + EPSILON) / (prec_sq + EPSILON)))
    scaled = (precond * ratio).astype(jnp.bfloat16)
    returned = lax.all_to_all(scaled[None], "fsdp", split_axis=1, concat_axis=0, tiled=True)
    update = jnp.einsum(
        "bs,srw->brw", placing, returned, preferred_element_type=jnp.float32
    ).astype(jnp.bfloat16)
    return (left_new[None], right_new[None], update)


def solution(mesh):
    in_specs = (
        P("rep", None, "fsdp", None),
        P(),
        P(),
        P("fsdp", "rep", None),
        P("fsdp", "rep", None),
        P("fsdp", "rep", None),
        P("fsdp", "rep", None),
    )
    out_specs = (P("fsdp", "rep", None), P("fsdp", "rep", None), P(None, ("rep", "fsdp"), None))
    return jax.shard_map(
        on_device, mesh=mesh, in_specs=in_specs, out_specs=out_specs, check_vma=False
    )
```

profile of v0, /device:TPU:0, one launch (start us, length us, event | category | flops | bytes accessed | tf_op | source)
XLA Modules:
  0.0 352.6 jit_solution(14322082575381790667)
XLA Ops:
  0.6 3.0 convolution_convert_fusion.1
  3.6 3.5 copy.33
  7.1 7.6 %all-to-all-start = ((bf16[32,40,1280]{2,1,0:T(8,128)(2,1)}), bf16[32,40,1280]{2,1,0:T(8,128)(2,1)}, u32[]{:S(2)}, u32[]{:S(2)}) async-start(bf16[32,40,1280]{2,1,0:T(8,128)(2,1)} %copy.33), calls=%async_computation | async-start | bytes 6553600 | tf_op jit(solution)/shard_map/all_to_all | solution.py:21
  14.8 0.2 reduce-window.8
  15.0 0.2 fusion.18
  15.2 73.6 %all-to-all-done = bf16[32,40,1280]{2,1,0:T(8,128)(2,1)} async-done(((bf16[32,40,1280]{2,1,0:T(8,128)(2,1)}), bf16[32,40,1280]{2,1,0:T(8,128)(2,1)}, u32[]{:S(2)}, u32[]{:S(2)}) %all-to-all-start) | async-done | bytes 3276832 | tf_op jit(solution)/shard_map/all_to_all | solution.py:21
  88.7 23.4 %multiply_reduce_fusion = (f32[]{:T(128)}, f32[1280,1280]{1,0:T(8,128)}) fusion(bf16[1,1280,1280]{2,1,0:T(8,128)(2,1)S(1)} %copy-done, bf16[1280,1280]{1,0:T(8,128)(2,1)} %bitcast.3, bf16[1,1280,1280]{2,1,0:T(8,128)(2,1)} %param.12), kind=kOutput, calls=%fused_computation.9 | convolution fusion | flops 8393523200 | bytes 16384004 | tf_op jit(solution)/shard_map/dot_general | solution.py:34
  112.1 4.2 %multiply_reduce_fusion.1 = f32[]{:T(128)} fusion(bf16[32,40,1280]{2,1,0:T(8,128)(2,1)} %all-to-all-done), kind=kLoop, calls=%fused_computation.10 | loop fusion | flops 4915199 | bytes 3276804 | tf_op jit(solution)/shard_map/reduce_sum | solution.py:44
  116.3 1.3 broadcast_multiply_fusion.1
  117.6 38.1 %all-reduce = (f32[2]{0:T(128)S(1)}, f32[2]{0:T(128)S(1)}) all-reduce(f32[2]{0:T(128)S(1)} %get-tuple-element.21, f32[2]{0:T(128)S(1)} %get-tuple-element.20), channel_id=1, replica_groups=mesh['rep'=1,'fsdp'=32] {'rep','fsdp'}, use_global_device_ids=true, to_apply=%region_5.6 | all-reduce | flops 4 | bytes 32 | tf_op jit(solution)/shard_map/psum | solution.py:46
  155.7 0.6 multiply_reduce_fusion.2
  156.3 4.0 %fusion.5 = bf16[1,1280,1280]{2,1,0:T(8,128)(2,1)S(1)} fusion(f32[1280,1280]{1,0:T(8,128)} %get-tuple-element.23, f32[]{:T(128)} %multiply_reduce_fusion.2), kind=kLoop, calls=%fused_computation.13 | loop fusion | flops 3276800 | bytes 9830404 | tf_op jit(solution)/shard_map/broadcast_in_dim | solution.py:49
  160.3 21.5 %copy.43 = bf16[1,1280,1280]{2,0,1:T(2,128)(2,1)} copy(bf16[1,1280,1280]{2,1,0:T(8,128)(2,1)S(1)} %fusion.5) | data formatting | bytes 6553600 | tf_op jit(solution)/shard_map/broadcast_in_dim | solution.py:49
  181.8 0.5 broadcast.28
  182.3 69.6 %reduce.1 = bf16[1280,1280]{1,0:T(8,128)(2,1)S(1)} reduce(bf16[1280,1,1280]{2,1,0:T(2,128)(2,1)} %bitcast.49, bf16[]{:T(256)} %broadcast.28), dimensions={1}, to_apply=%bitcast.48.reduce_sub_computation | reduce | bytes 6553602
  251.8 2.5 reshape.47
  254.4 5.3 %all-to-all-start.1 = ((bf16[32,2,25600]{2,1,0:T(2,128)(2,1)}), bf16[32,2,25600]{2,1,0:T(2,128)(2,1)S(1)}, u32[]{:S(2)}, u32[]{:S(2)}) async-start(bf16[32,2,25600]{2,1,0:T(2,128)(2,1)} %reshape.47), calls=%async_computation.1 | async-start | bytes 6553600 | tf_op jit(solution)/shard_map/all_to_all | solution.py:49
  259.7 12.2 %fusion.1 = f32[1,1280,1280]{2,1,0:T(8,128)} fusion(bf16[1280,1280]{1,0:T(8,128)(2,1)} %bitcast.3, f32[1,1280,1280]{2,1,0:T(8,128)} %param.10), kind=kOutput, calls=%fused_computation.2 | convolution fusion | flops 4199219200 | bytes 16384000 | tf_op jit(solution)/shard_map/dot_general | solution.py:26
  271.9 12.3 %fusion.4 = f32[1,1280,1280]{2,1,0:T(8,128)} fusion(bf16[32,40,1280]{2,1,0:T(8,128)(2,1)} %all-to-all-done, f32[1,1280,1280]{2,1,0:T(8,128)} %param.11), kind=kOutput, calls=%fused_computation.6 | convolution fusion | flops 4199219200 | bytes 16384000 | tf_op jit(solution)/shard_map/dot_general | solution.py:27
  284.2 49.6 %all-to-all-done.1 = bf16[32,2,25600]{2,1,0:T(2,128)(2,1)S(1)} async-done(((bf16[32,2,25600]{2,1,0:T(2,128)(2,1)}), bf16[32,2,25600]{2,1,0:T(2,128)(2,1)S(1)}, u32[]{:S(2)}, u32[]{:S(2)}) %all-to-all-start.1) | async-done | bytes 3276832 | tf_op jit(solution)/shard_map/all_to_all | solution.py:49
  333.8 12.3 %reshape.48 = bf16[1280,1,1280]{2,1,0:T(2,128)(2,1)} reshape(bf16[32,2,25600]{2,1,0:T(2,128)(2,1)S(1)} %all-to-all-done.1) | data formatting | bytes 6553600
  346.1 3.4 copy.37
  349.5 0.9 convolution_convert_fusion.2
  350.3 1.9 copy.36
  (10 shorter events, 0.0 us)
Async XLA Ops:
  0.6 88.1 %copy-start = (bf16[1,1280,1280]{2,1,0:T(8,128)(2,1)S(1)}, bf16[1,1280,1280]{2,1,0:T(8,128)(2,1)}, u32[]{:S(2)}) copy-start(bf16[1,1280,1280]{2,1,0:T(8,128)(2,1)} %param.13) | copy-start | bytes 9830404
  7.1 7.6 %copy-start.3 = (s32[2]{0:T(128)S(1)}, s32[2]{0:T(128)}, u32[]{:S(2)}) copy-start(s32[2]{0:T(128)} %param.8) | copy-start | bytes 28
  7.1 7.8 %copy-start.2 = (s32[24]{0:T(128)S(1)}, s32[24]{0:T(128)}, u32[]{:S(2)}) copy-start(s32[24]{0:T(128)} %param.9) | copy-start | bytes 292
  7.1 81.6 %all-to-all-start = ((bf16[32,40,1280]{2,1,0:T(8,128)(2,1)}), bf16[32,40,1280]{2,1,0:T(8,128)(2,1)}, u32[]{:S(2)}, u32[]{:S(2)}) async-start(bf16[32,40,1280]{2,1,0:T(8,128)(2,1)} %copy.33), calls=%async_computation | async-start | bytes 6553600 | tf_op jit(solution)/shard_map/all_to_all | solution.py:21
  254.4 79.4 %all-to-all-start.1 = ((bf16[32,2,25600]{2,1,0:T(2,128)(2,1)}), bf16[32,2,25600]{2,1,0:T(2,128)(2,1)S(1)}, u32[]{:S(2)}, u32[]{:S(2)}) async-start(bf16[32,2,25600]{2,1,0:T(2,128)(2,1)} %reshape.47), calls=%async_computation.1 | async-start | bytes 6553600 | tf_op jit(solution)/shard_map/all_to_all | solution.py:49
  349.4 2.8 copy-start.1
where the time goes:
time: 356 us; the launch traced here: 353 us
  waiting for transfers between devices  123 us (35%)
  other arithmetic  80 us (22%)
  matrix products  51.7 us (15%)
  local copies, waits for them, and re-layouts  45.6 us (13%)
  blocking collectives  38.1 us (11%)
  starting transfers between devices  12.9 us (4%)
    all_to_all x1, waiting for transfers between devices, on_device(): lax.all_to_all(slotted, 'fsdp', split_axis=0, concat_axis=1, tiled=True)[0]  73.6 us
    unnamed x1, other arithmetic  69.6 us
    all_to_all x1, waiting for transfers between devices, on_device(): lax.all_to_all(scaled[None], 'fsdp', split_axis=1, concat_axis=0, tiled=T...  49.6 us
    psum x1, blocking collectives, on_device(): grad_sq, prec_sq = lax.psum((grad_part, prec_part), ('rep', 'fsdp'))  38.1 us
    dot_general x1, matrix products, on_device(): precond = jnp.dot(halfway, whole_root, preferred_element_type=jnp.float32)  23.4 us
    broadcast_in_dim x1, local copies, waits for them, and re-layouts, on_device(): scaled[None]  21.5 us
    unnamed x13, local copies, waits for them, and re-layouts  20.6 us
    dot_general x1, matrix products, on_device(): lax.dot_general(columns, block, (((0,), (0,)), ((), ())), preferred_eleme...  12.3 us
  transfers between devices with their start and end apart: 2, of which 2 were waited for; matrix products, arithmetic and copies ran while one was open for 7% of the time, Pallas kernels for 0%

commit v1 on v0

--- a/solution.py
+++ b/solution.py
@@ -18,7 +18,9 @@
     slotted = jnp.einsum("bs,brc->src", placing, summed, preferred_element_type=jnp.float32).astype(
         jnp.bfloat16
     )
-    block = lax.all_to_all(slotted, "fsdp", split_axis=0, concat_axis=1, tiled=True)[0]
+    rows = local.shape[1]
+    block = lax.all_to_all(slotted, "fsdp", split_axis=0, concat_axis=0, tiled=True)
+    block = block.reshape(slots * rows, width)
     first = lax.axis_index("rep") * half_rows
     mine = lax.dynamic_slice_in_dim(block, first, half_rows, 0)
     columns = lax.dynamic_slice_in_dim(block, first, half_rows, 1)
@@ -46,7 +48,8 @@
     grad_sq, prec_sq = lax.psum((grad_part, prec_part), ("rep", "fsdp"))
     ratio = jnp.sum(my_groups * jnp.sqrt((grad_sq + EPSILON) / (prec_sq + EPSILON)))
     scaled = (precond * ratio).astype(jnp.bfloat16)
-    returned = lax.all_to_all(scaled[None], "fsdp", split_axis=1, concat_axis=0, tiled=True)
+    pieces = scaled.reshape(slots, half_rows // slots, width)
+    returned = lax.all_to_all(pieces, "fsdp", split_axis=0, concat_axis=0, tiled=True)
     update = jnp.einsum(
         "bs,srw->brw", placing, returned, preferred_element_type=jnp.float32
     ).astype(jnp.bfloat16)

time: 356 us -> 246 us (0.69)
  other arithmetic: 80 us -> 12.2 us
  local copies, waits for them, and re-layouts: 45.6 us -> 5.4 us
    unnamed x1 -> x0, other arithmetic: 69.6 us -> none
    broadcast_in_dim x1 -> x0, local copies, waits for them, and re-layouts: 21.5 us -> none  [on_device(): scaled[None]]
    unnamed x13 -> x7, local copies, waits for them, and re-layouts: 20.6 us -> 1.9 us
    convert_element_type x0 -> x1, other arithmetic: none -> 5.75 us  [on_device(): scaled = (precond * ratio).astype(jnp.bfloat16)]
    broadcast_in_dim x1 -> x0, other arithmetic: 4 us -> none  [on_device(): scaled[None]]
  transfers between devices with their start and end apart: 2 -> 2, of which waited for: 2 -> 2; matrix products, arithmetic and copies ran while one was open for 7% -> 10% of each run, Pallas kernels for 0% -> 0%
where the time goes in v1:
time: 246 us
  waiting for transfers between devices  123 us (50%)
  matrix products  53.6 us (22%)
  blocking collectives  38.1 us (15%)
  starting transfers between devices  12.7 us (5%)
  other arithmetic  12.2 us (5%)
  local copies, waits for them, and re-layouts  5.4 us (2%)
    all_to_all x1, waiting for transfers between devices, on_device(): lax.all_to_all(slotted, 'fsdp', split_axis=0, concat_axis=0, tiled=True)  73.6 us
    all_to_all x1, waiting for transfers between devices, on_device(): lax.all_to_all(pieces, 'fsdp', split_axis=0, concat_axis=0, tiled=True)  49.6 us
    psum x1, blocking collectives, on_device(): grad_sq, prec_sq = lax.psum((grad_part, prec_part), ('rep', 'fsdp'))  38.1 us
    dot_general x1, matrix products, on_device(): precond = jnp.dot(halfway, whole_root, preferred_element_type=jnp.float32)  23.4 us
    dot_general x1, matrix products, on_device(): lax.dot_general(columns, block, (((0,), (0,)), ((), ())), preferred_eleme...  12.3 us
    dot_general x1, matrix products, on_device(): left_gram = jnp.dot(mine, block.T, preferred_element_type=jnp.float32)  12.2 us
    all_to_all x1, starting transfers between devices, on_device(): lax.all_to_all(slotted, 'fsdp', split_axis=0, concat_axis=0, tiled=True)  7.62 us
    convert_element_type x1, other arithmetic, on_device(): scaled = (precond * ratio).astype(jnp.bfloat16)  5.75 us
  transfers between devices with their start and end apart: 2, of which 2 were waited for; matrix products, arithmetic and copies ran while one was open for 10% of the time, Pallas kernels for 0%

profile of v1, /device:TPU:0, one launch (start us, length us, event | category | flops | bytes accessed | tf_op | source)
XLA Modules:
  0.0 246.0 jit_solution(1293500548713548406)
XLA Ops:
  0.6 0.0 copy-start
  0.6 3.0 %convolution_convert_fusion.1 = bf16[32,40,1280]{2,0,1:T(8,128)(2,1)S(1)} fusion(bf16[24,40,1280]{2,1,0:T(8,128)(2,1)} %bitcast.44, s32[24]{0:T(128)} %param.9), kind=kOutput, calls=%fused_computation.11 | convolution fusion | flops 80282368 | bytes 5734496 | tf_op jit(solution)/shard_map/bs,brc->src/dot_general | solution.py:18
  3.6 3.5 %copy.28 = bf16[32,40,1280]{2,1,0:T(8,128)(2,1)} copy(bf16[32,40,1280]{2,0,1:T(8,128)(2,1)S(1)} %convolution_convert_fusion.1) | data formatting | bytes 6553600 | tf_op jit(solution)/shard_map/convert_element_type | solution.py:18
  7.1 0.0 copy-start.2
  7.1 0.0 copy-start.1
  7.1 7.6 %all-to-all-start = ((bf16[32,40,1280]{2,1,0:T(8,128)(2,1)}), bf16[32,40,1280]{2,1,0:T(8,128)(2,1)}, u32[]{:S(2)}, u32[]{:S(2)}) async-start(bf16[32,40,1280]{2,1,0:T(8,128)(2,1)} %copy.28), calls=%async_computation | async-start | bytes 6553600 | tf_op jit(solution)/shard_map/all_to_all | solution.py:22
  14.8 0.0 copy-done.2
  14.8 0.2 reduce-window.8
  15.0 0.0 copy-done.1
  15.0 0.2 fusion.17
  15.2 73.6 %all-to-all-done = bf16[32,40,1280]{2,1,0:T(8,128)(2,1)} async-done(((bf16[32,40,1280]{2,1,0:T(8,128)(2,1)}), bf16[32,40,1280]{2,1,0:T(8,128)(2,1)}, u32[]{:S(2)}, u32[]{:S(2)}) %all-to-all-start) | async-done | bytes 3276832 | tf_op jit(solution)/shard_map/all_to_all | solution.py:22
  88.7 0.0 copy-done
  88.7 23.4 %multiply_reduce_fusion = (f32[]{:T(128)}, f32[1280,1280]{1,0:T(8,128)}) fusion(bf16[1,1280,1280]{2,1,0:T(8,128)(2,1)S(1)} %copy-done, bf16[1280,1280]{1,0:T(8,128)(2,1)} %bitcast.3, bf16[1,1280,1280]{2,1,0:T(8,128)(2,1)} %param.12), kind=kOutput, calls=%fused_computation.9 | convolution fusion | flops 8393523200 | bytes 16384004 | tf_op jit(solution)/shard_map/dot_general | solution.py:36
  112.1 4.2 %multiply_reduce_fusion.1 = f32[]{:T(128)} fusion(bf16[32,40,1280]{2,1,0:T(8,128)(2,1)} %all-to-all-done), kind=kLoop, calls=%fused_computation.10 | loop fusion | flops 4915199 | bytes 3276804 | tf_op jit(solution)/shard_map/reduce_sum | solution.py:46
  116.3 1.3 broadcast_multiply_fusion.1
  117.6 38.1 %all-reduce = (f32[2]{0:T(128)S(1)}, f32[2]{0:T(128)S(1)}) all-reduce(f32[2]{0:T(128)S(1)} %get-tuple-element.18, f32[2]{0:T(128)S(1)} %get-tuple-element.17), channel_id=1, replica_groups=mesh['rep'=1,'fsdp'=32] {'rep','fsdp'}, use_global_device_ids=true, to_apply=%region_5.6 | all-reduce | flops 4 | bytes 32 | tf_op jit(solution)/shard_map/psum | solution.py:48
  155.7 0.6 multiply_reduce_fusion.2
  156.3 5.7 %multiply_convert_fusion = bf16[1280,1280]{1,0:T(8,128)(2,1)} fusion(f32[1280,1280]{1,0:T(8,128)} %get-tuple-element.20, f32[]{:T(128)} %multiply_reduce_fusion.2), kind=kLoop, calls=%fused_computation.8 | loop fusion | flops 3276800 | bytes 9830404 | tf_op jit(solution)/shard_map/convert_element_type | solution.py:50
  162.0 5.1 %all-to-all-start.1 = ((bf16[32,40,1280]{2,1,0:T(8,128)(2,1)}), bf16[32,40,1280]{2,1,0:T(8,128)(2,1)}, u32[]{:S(2)}, u32[]{:S(2)}) async-start(bf16[32,40,1280]{2,1,0:T(8,128)(2,1)} %bitcast.43), calls=%async_computation.1 | async-start | bytes 6553600 | tf_op jit(solution)/shard_map/all_to_all | solution.py:52
  167.2 12.2 %fusion.1 = f32[1,1280,1280]{2,1,0:T(8,128)} fusion(bf16[1280,1280]{1,0:T(8,128)(2,1)} %bitcast.3, f32[1,1280,1280]{2,1,0:T(8,128)} %param.10), kind=kOutput, calls=%fused_computation.2 | convolution fusion | flops 4199219200 | bytes 16384000 | tf_op jit(solution)/shard_map/dot_general | solution.py:28
  179.4 12.3 %fusion.4 = f32[1,1280,1280]{2,1,0:T(8,128)} fusion(bf16[32,40,1280]{2,1,0:T(8,128)(2,1)} %all-to-all-done, f32[1,1280,1280]{2,1,0:T(8,128)} %param.11), kind=kOutput, calls=%fused_computation.6 | convolution fusion | flops 4199219200 | bytes 16384000 | tf_op jit(solution)/shard_map/dot_general | solution.py:29
  191.7 49.6 %all-to-all-done.1 = bf16[32,40,1280]{2,1,0:T(8,128)(2,1)} async-done(((bf16[32,40,1280]{2,1,0:T(8,128)(2,1)}), bf16[32,40,1280]{2,1,0:T(8,128)(2,1)}, u32[]{:S(2)}, u32[]{:S(2)}) %all-to-all-start.1) | async-done | bytes 3276832 | tf_op jit(solution)/shard_map/all_to_all | solution.py:52
  241.3 2.8 %convolution_convert_fusion.2 = bf16[24,40,1280]{2,0,1:T(8,128)(2,1)S(1)} fusion(bf16[32,40,1280]{2,1,0:T(8,128)(2,1)} %all-to-all-done.1, s32[24]{0:T(128)S(1)} %copy-done.1), kind=kOutput, calls=%fused_computation.12 | convolution fusion | flops 79872768 | bytes 5734496 | tf_op jit(solution)/shard_map/bs,srw->brw/dot_general | solution.py:53
  244.1 1.9 copy.30
  (2 shorter events, 0.0 us)
Async XLA Ops:
  0.6 88.1 %copy-start = (bf16[1,1280,1280]{2,1,0:T(8,128)(2,1)S(1)}, bf16[1,1280,1280]{2,1,0:T(8,128)(2,1)}, u32[]{:S(2)}) copy-start(bf16[1,1280,1280]{2,1,0:T(8,128)(2,1)} %param.13) | copy-start | bytes 9830404
  7.1 7.6 %copy-start.2 = (s32[2]{0:T(128)S(1)}, s32[2]{0:T(128)}, u32[]{:S(2)}) copy-start(s32[2]{0:T(128)} %param.8) | copy-start | bytes 28
  7.1 7.8 %copy-start.1 = (s32[24]{0:T(128)S(1)}, s32[24]{0:T(128)}, u32[]{:S(2)}) copy-start(s32[24]{0:T(128)} %param.9) | copy-start | bytes 292
  7.1 81.6 %all-to-all-start = ((bf16[32,40,1280]{2,1,0:T(8,128)(2,1)}), bf16[32,40,1280]{2,1,0:T(8,128)(2,1)}, u32[]{:S(2)}, u32[]{:S(2)}) async-start(bf16[32,40,1280]{2,1,0:T(8,128)(2,1)} %copy.28), calls=%async_computation | async-start | bytes 6553600 | tf_op jit(solution)/shard_map/all_to_all | solution.py:22
  162.0 79.3 %all-to-all-start.1 = ((bf16[32,40,1280]{2,1,0:T(8,128)(2,1)}), bf16[32,40,1280]{2,1,0:T(8,128)(2,1)}, u32[]{:S(2)}, u32[]{:S(2)}) async-start(bf16[32,40,1280]{2,1,0:T(8,128)(2,1)} %bitcast.43), calls=%async_computation.1 | async-start | bytes 6553600 | tf_op jit(solution)/shard_map/all_to_all | solution.py:52
